TPU v7x, 32 devices: a whole 2x2x4 slice. The times are simulated.
32 devices in a mesh: rep: 2 (over x), dp: 16 (over y, z, core).
Axes of the slice: x: 2, y: 2, z: 4, core: 2. Of those that a mesh axis runs over, the one named last changes fastest.
Arguments:
- a: bfloat16 [32, 4, 8192, 1024], P(('rep', 'dp')), parts along dimension 0
- g: bfloat16 [32, 4, 8192, 2816], P(('rep', 'dp')), parts along dimension 0
Outputs:
- output: bfloat16 [8, 1024, 2816], P('rep'), parts along dimension 0
There are 2 independent parts. A program takes and returns all parts, laid end to end along the dimension named above; each array names one.
All inputs are finite; a program needn't handle non-finite values.
Results may differ from a plain program's by a relative error of at most 0.012.
Values are sent between devices in bfloat16 or wider.
A program may use at most 2 GiB of HBM per device.

v0:
```python
import jax
import jax.numpy as jnp


def solution(mesh):
    groups = mesh.shape["rep"]

    def step(a, g):
        a, g = (t.reshape(groups, -1, *t.shape[1:]) for t in (a, g))
        sums = jnp.einsum("rsntd,rsntf->rndf", a, g, preferred_element_type=jnp.float32)
        return sums.astype(jnp.bfloat16).reshape(-1, *sums.shape[2:])

    return step
```

profile of v0, /device:TPU:0, one launch (start us, length us, event | category | flops | bytes accessed | tf_op | source)
XLA Modules:
  0.0 1162.9 jit_solution(3519788184387877624)
XLA Ops:
  0.0 211.9 %fusion.3 = f32[1,4,1024,2816]{3,2,1,0:T(8,128)} fusion(bf16[1,4,8192,2816]{3,2,1,0:T(8,128)(2,1)} %param.1, bf16[1,4,8192,1024]{3,2,1,0:T(8,128)(2,1)} %param), kind=kOutput, calls=%fused_computation.3 | convolution fusion | flops 188978561024 | bytes 297795584 | tf_op jit(solution)/rsntd,rsntf->rndf/dot_general | solution.py:10
  211.9 951.1 %all-reduce.2 = bf16[1,4,1024,2816]{3,2,1,0:T(8,128)(2,1)} all-reduce(f32[1,4,1024,2816]{3,2,1,0:T(8,128)} %fusion.3), channel_id=1, replica_groups=[2,16]<=[32], use_global_device_ids=true, to_apply=%add.clone | all-reduce | flops 11534336 | bytes 69206016 | tf_op jit(solution)/rsntd,rsntf->rndf/dot_general | solution.py:10
where the time goes:
time: 1160 us
  blocking collectives  951 us (82%)
  matrix products  212 us (18%)
    dot_general x1, blocking collectives, step(): jnp.einsum('rsntd,rsntf->rndf', a, g, preferred_element_type=jnp.float32)  951 us
    dot_general x1, matrix products, step(): jnp.einsum('rsntd,rsntf->rndf', a, g, preferred_element_type=jnp.float32)  212 us

commit v1 on v0

v1 whole, which is shorter than its diff:
```python
import functools

import jax
import jax.numpy as jnp
from jax import lax
from jax.experimental import pallas as pl
from jax.experimental.pallas import tpu as pltpu
from jax.sharding import PartitionSpec as P

CW = 256
LAG = (1, 3, 5, 7, 9, 11, 13, 15)
WL = 16
WS = 8
WF = 4
VMEM_LIMIT = 67043328
F32, BF16 = jnp.float32, jnp.bfloat16


def kernel(a, g, out, av, gv, acc, s0s, s0r, sbuf, ra, rb, rc, fbuf,
           a_sem, g_sem, s0_ssem, s0_rsem, r_ssem, ra_sem, rb_sem, rc_sem, b_ssem, b_rsem, p_rsem):
    matrices, tokens, depth = a.shape
    per = g.shape[2] // CW
    blocks = matrices * per
    q = depth // 8
    half, quarter = 4 * q, 2 * q

    me = lax.axis_index("dp")
    core, z, y = me % 2, (me // 2) % 4, me // 8
    zi = z // 2
    mid = jnp.logical_or(z == 1, z == 2)
    end = jnp.logical_not(mid)
    yf, zf = core == 0, core == 1
    partner = me + 1 - 2 * core
    across = me + 8 - 16 * y
    side = me + 2 - 4 * (z % 2)
    other = me + 2 * (3 - 2 * z)

    def both(*conditions):
        return functools.reduce(jnp.logical_and, conditions)

    def rows(start, size):
        return pl.ds(pl.multiple_of(start, q), size)

    def piece(r, zz):
        return core * half + r * (quarter - q * core) + zz * (q + q * core)

    def place(j, start, size=q):
        columns = pl.ds(pl.multiple_of((j % per) * CW, CW), CW)
        return out.at[j // per, rows(start, size), columns]

    def remote(src, dst, ssem, rsem, to):
        return pltpu.make_async_remote_copy(
            src_ref=src, dst_ref=dst, send_sem=ssem, recv_sem=rsem,
            device_id={"dp": to}, device_id_type=pl.DeviceIdType.MESH)

    def a_load(n):
        return pltpu.make_async_copy(a.at[n], av.at[n % 2], a_sem.at[n % 2])

    def g_load(i):
        columns = pl.ds(pl.multiple_of((i % per) * CW, CW), CW)
        return pltpu.make_async_copy(g.at[i // per, :, columns], gv.at[i % 2], g_sem.at[i % 2])

    def s0(i):
        return remote(s0s.at[i % WF], s0r.at[i % WF], s0_ssem.at[i % WF], s0_rsem.at[i % WF], partner)

    def to_a(j, start, size, to, k):
        return remote(sbuf.at[j % WS, rows(start, size)], ra.at[j % WL, pl.ds(0, size)],
                      r_ssem.at[k, j % WF], ra_sem.at[j % WL], to)

    def to_b(j, start, to, k):
        return remote(sbuf.at[j % WS, rows(start, quarter)], rb.at[j % WS],
                      r_ssem.at[k, j % WF], rb_sem.at[j % WS], to)

    def to_c(j, start, to):
        return remote(sbuf.at[j % WS, rows(start, q)], rc.at[j % WS],
                      r_ssem.at[2, j % WF], rc_sem.at[j % WS], to)

    def finished(j, r, zz, slot, kind, to, src=None):
        at = place(j, piece(r, zz))
        return remote(at if src is None else src, at, b_ssem.at[slot, j % WF], b_rsem.at[kind, j % WL], to)

    def beside(j, r, zz, slot, src=None):
        at = place(j, piece(r, zz))
        return remote(at if src is None else src, at, b_ssem.at[slot, j % WF], p_rsem.at[r * 2 + zz, j % WL], partner)

    def arrived(j, r, zz, kind):
        finished(j, r, zz, 0, kind, partner).wait_recv()

    def sent(j, *slots):
        for slot in slots:
            finished(j, 0, 0, slot, 0, partner).wait_send()

    def mine(j, start, size):
        return acc.at[j % WS, rows(core * half + start, size)]

    def plus(x, y):
        return x[...] + y[...].astype(F32)

    def multiply(i):
        g_load(i).wait()

        @pl.when(i % per == 0)
        def _():
            a_load(i // per).wait()

        @pl.when(both(i % per == 0, i // per + 1 < matrices))
        def _():
            a_load(i // per + 1).start()

        acc[i % WS] = lax.dot_general(av[(i // per) % 2], gv[i % 2], (((0,), (0,)), ((), ())),
                                      preferred_element_type=F32)
        s0s[i % WF] = acc[i % WS, rows((1 - core) * half, half)].astype(BF16)

        @pl.when(i + 2 < blocks)
        def _():
            g_load(i + 2).start()

        s0(i).start()

    def stage1(j):
        s0(j).wait()
        theirs = s0r.at[j % WF]

        @pl.when(yf)
        def _():
            away, own = (1 - y) * quarter, y * quarter
            sbuf[j % WS, rows(away, quarter)] = plus(mine(j, away, quarter), theirs.at[rows(away, quarter)]).astype(BF16)
            to_b(j, away, across, 0).start()
            mine(j, own, quarter)[...] = plus(mine(j, own, quarter), theirs.at[rows(own, quarter)])

        @pl.when(both(zf, end))
        def _():
            sbuf[j % WS] = plus(mine(j, 0, half), theirs).astype(BF16)
            to_a(j, 0, half, side, 0).start()

        @pl.when(both(zf, mid))
        def _():
            mine(j, 0, half)[...] = plus(mine(j, 0, half), theirs)

    def stage2(j):
        @pl.when(yf)
        def _():
            own = y * quarter
            to_b(j, (1 - y) * quarter, across, 0).wait()

            @pl.when(end)
            def _():
                sbuf[j % WS, rows(own, quarter)] = plus(mine(j, own, quarter), rb.at[j % WS]).astype(BF16)
                to_a(j, own, quarter, side, 1).start()

            @pl.when(mid)
            def _():
                mine(j, own, quarter)[...] = plus(mine(j, own, quarter), rb.at[j % WS])

        @pl.when(both(zf, end))
        def _():
            to_a(j, 0, half, side, 0).wait_send()

        @pl.when(both(zf, mid))
        def _():
            to_a(j, 0, half, side, 0).wait_recv()
            away, own = (1 - zi) * quarter, zi * quarter
            theirs = ra.at[j % WL]
            sbuf[j % WS, rows(away, quarter)] = plus(mine(j, away, quarter), theirs.at[rows(away, quarter)]).astype(BF16)
            to_b(j, away, other, 1).start()
            mine(j, own, quarter)[...] = plus(mine(j, own, quarter), theirs.at[rows(own, quarter)])

    def stage3(j):
        @pl.when(both(yf, end))
        def _():
            to_a(j, y * quarter, quarter, side, 1).wait_send()

        @pl.when(both(yf, mid))
        def _():
            to_a(j, y * quarter, quarter, side, 1).wait_recv()
            away, own = (1 - zi) * q, zi * q
            theirs = ra.at[j % WL]
            sbuf[j % WS, rows(y * quarter + away, q)] = plus(
                mine(j, y * quarter + away, q), theirs.at[rows(away, q)]).astype(BF16)
            to_c(j, y * quarter + away, other).start()
            mine(j, y * quarter + own, q)[...] = plus(mine(j, y * quarter + own, q), theirs.at[rows(own, q)])

        @pl.when(both(zf, mid))
        def _():
            to_b(j, (1 - zi) * quarter, other, 1).wait()
            away, own = (1 - y) * q, y * q
            theirs = rb.at[j % WS]
            sbuf[j % WS, rows(zi * quarter + away, q)] = plus(
                mine(j, zi * quarter + away, q), theirs.at[rows(away, q)]).astype(BF16)
            to_c(j, zi * quarter + away, across).start()
            mine(j, zi * quarter + own, q)[...] = plus(mine(j, zi * quarter + own, q), theirs.at[rows(own, q)])

    def stage4(j):
        @pl.when(mid)
        def _():
            to_c(j, 0, partner).wait()
            f = fbuf.at[j % WF]
            f[...] = plus(acc.at[j % WS, rows(piece(y, zi), q)], rc.at[j % WS]).astype(BF16)
            finished(j, y, zi, 0, 0, other, f).start()
            finished(j, y, zi, 1, 1, across, f).start()
            finished(j, y, zi, 2, 0, side, f).start()
            beside(j, y, zi, 3, f).start()
            pltpu.make_async_copy(f, place(j, piece(y, zi)), b_ssem.at[4, j % WF]).start()

    def stage5(j):
        @pl.when(mid)
        def _():
            sent(j, 0, 1, 2, 3)
            pltpu.make_async_copy(fbuf.at[j % WF], place(j, piece(y, zi)), b_ssem.at[4, j % WF]).wait()
            arrived(j, y, 1 - zi, 0)

            @pl.when(yf)
            def _():
                finished(j, y, 1 - zi, 5, 1, side).start()
                finished(j, y, 1 - zi, 6, 2, across).start()

            @pl.when(zf)
            def _():
                finished(j, y, 1 - zi, 5, 2, side).start()

            beside(j, y, 1 - zi, 7).start()
            arrived(j, 1 - y, zi, 1)

            @pl.when(zf)
            def _():
                finished(j, 1 - y, zi, 6, 2, other).start()
                finished(j, 1 - y, zi, 9, 1, side).start()

            beside(j, 1 - y, zi, 8).start()

        @pl.when(end)
        def _():
            arrived(j, y, zi, 0)

            @pl.when(yf)
            def _():
                finished(j, y, zi, 6, 2, across).start()

            beside(j, y, zi, 5).start()

    def stage6(j):
        @pl.when(mid)
        def _():
            sent(j, 5, 6, 7, 8)

            @pl.when(zf)
            def _():
                sent(j, 9)

            arrived(j, 1 - y, 1 - zi, 2)

            @pl.when(zf)
            def _():
                finished(j, 1 - y, 1 - zi, 11, 3, side).start()

            beside(j, 1 - y, 1 - zi, 10).start()

        @pl.when(end)
        def _():
            sent(j, 5)

        @pl.when(both(end, yf))
        def _():
            sent(j, 6)
            arrived(j, y, 1 - zi, 1)
            finished(j, y, 1 - zi, 11, 3, across).start()
            beside(j, y, 1 - zi, 10).start()
            arrived(j, 1 - y, zi, 2)
            beside(j, 1 - y, zi, 12).start()

        @pl.when(both(end, zf))
        def _():
            arrived(j, 1 - y, zi, 1)
            beside(j, 1 - y, zi, 10).start()
            arrived(j, y, 1 - zi, 2)
            beside(j, y, 1 - zi, 12).start()

    def stage7(j):
        sent(j, 10)

        @pl.when(both(zf, mid))
        def _():
            sent(j, 11)

        @pl.when(both(yf, end))
        def _():
            sent(j, 11)

        @pl.when(end)
        def _():
            sent(j, 12)
            arrived(j, 1 - y, 1 - zi, 3)
            beside(j, 1 - y, 1 - zi, 13).start()

    def stage8(j):
        @pl.when(end)
        def _():
            sent(j, 13)

        for k in range(4):
            beside(j, k // 2, k % 2, 0).wait_recv()

    a_load(0).start()
    g_load(0).start()
    g_load(1).start()

    barrier = pltpu.get_barrier_semaphore()

    def hello(to):
        pl.semaphore_signal(barrier, inc=1, device_id={"dp": to}, device_id_type=pl.DeviceIdType.MESH)

    for to in (partner, across, side):
        hello(to)

    @pl.when(mid)
    def _():
        hello(other)
        pl.semaphore_wait(barrier, 4)

    @pl.when(end)
    def _():
        pl.semaphore_wait(barrier, 3)

    stages = (stage1, stage2, stage3, stage4, stage5, stage6, stage7, stage8)

    def tick(i, carry):
        @pl.when(i < blocks)
        def _():
            multiply(i)

        for stage, lag in zip(stages, LAG):
            pl.when(both(i >= lag, i < blocks + lag))(functools.partial(stage, i - lag))
        return carry

    lax.fori_loop(0, blocks + LAG[-1], tick, 0)


def solution(mesh):
    def step(a, g):
        _, matrices, tokens, depth = a.shape
        width = g.shape[3]
        q = depth // 8
        dma = pltpu.SemaphoreType.DMA
        return pl.pallas_call(
            kernel,
            out_shape=jax.ShapeDtypeStruct((matrices, depth, width), BF16),
            in_specs=[pl.BlockSpec(memory_space=pl.ANY)] * 2,
            out_specs=pl.BlockSpec(memory_space=pl.ANY),
            scratch_shapes=[
                pltpu.VMEM((2, tokens, depth), BF16),
                pltpu.VMEM((2, tokens, CW), BF16),
                pltpu.VMEM((WS, depth, CW), F32),
                pltpu.VMEM((WF, 4 * q, CW), BF16),
                pltpu.VMEM((WF, 4 * q, CW), BF16),
                pltpu.VMEM((WS, 4 * q, CW), BF16),
                pltpu.VMEM((WL, 4 * q, CW), BF16),
                pltpu.VMEM((WS, 2 * q, CW), BF16),
                pltpu.VMEM((WS, q, CW), BF16),
                pltpu.VMEM((WF, q, CW), BF16),
                dma((2,)), dma((2,)), dma((WF,)), dma((WF,)), dma((3, WF)), dma((WL,)), dma((WS,)), dma((WS,)),
                dma((14, WF)), dma((4, WL)), dma((4, WL)),
            ],
            compiler_params=pltpu.CompilerParams(
                collective_id=0, has_side_effects=True, vmem_limit_bytes=VMEM_LIMIT),
            cost_estimate=pl.CostEstimate(
                flops=2 * matrices * tokens * depth * width,
                bytes_accessed=2 * matrices * (tokens * (depth + width) + depth * width), transcendentals=0),
            name="sums",
        )(a[0], g[0])

    return jax.shard_map(
        step, mesh=mesh,
        in_specs=(P(("rep", "dp"), None, None, None),) * 2,
        out_specs=P("rep", None, None), check_vma=False)
```

time: 1160 us -> 297 us (0.26)
  blocking collectives: 951 us -> 0 us
  Pallas kernels: 0 us -> 277 us
  matrix products: 212 us -> 0 us
  local copies, waits for them, and re-layouts: 0 us -> 19.8 us
    dot_general x1 -> x0, blocking collectives: 951 us -> none  [step(): jnp.einsum('rsntd,rsntf->rndf', a, g, preferred_element_type=jnp.float32)]
    pallas_call x0 -> x1, Pallas kernels: none -> 277 us  [step(): pl.pallas_call(kernel, out_shape=jax.ShapeDtypeStruct((matrices, depth, w...]
    dot_general x1 -> x0, matrix products: 212 us -> none  [step(): jnp.einsum('rsntd,rsntf->rndf', a, g, preferred_element_type=jnp.float32)]
    unnamed x0 -> x1, local copies, waits for them, and re-layouts: none -> 19.8 us
where the time goes in v1:
time: 297 us
  Pallas kernels  277 us (93%)
  local copies, waits for them, and re-layouts  19.8 us (7%)
    pallas_call x1, Pallas kernels, step(): pl.pallas_call(kernel, out_shape=jax.ShapeDtypeStruct((matrices, depth, w...  277 us
    unnamed x1, local copies, waits for them, and re-layouts  19.8 us

profile of v1, /device:TPU:0, one launch (start us, length us, event | category | flops | bytes accessed | tf_op | source)
XLA Modules:
  0.0 296.9 jit_solution(6019014704060880319)
XLA Ops:
  0.0 277.1 %sums.1 = bf16[4,1024,2816]{2,1,0:T(8,128)(2,1)} custom-call(bf16[4,8192,1024]{2,1,0:T(8,128)(2,1)} %bitcast.a, bf16[4,8192,2816]{2,1,0:T(8,128)(2,1)} %bitcast.1.g), custom_call_target="tpu_custom_call" | custom-call | flops 188978561024 | bytes 274726912 | tf_op jit(solution)/shard_map/sums/pallas_call | solution.py:344
  277.1 19.8 %copy.4 = bf16[4,1024,2816]{2,1,0:T(8,128)(2,1)} copy(bf16[4,1024,2816]{2,1,0:T(8,128)(2,1)} %sums.1) | data formatting | bytes 46137344

commit v2 on v1

--- a/solution.py
+++ b/solution.py
@@ -8,7 +8,7 @@
 from jax.sharding import PartitionSpec as P
 
 CW = 256
-LAG = (1, 3, 5, 7, 9, 11, 13, 15)
+LAG = (1, 2, 3, 4, 5, 7, 9, 10)
 WL = 16
 WS = 8
 WF = 4
@@ -16,8 +16,11 @@
 F32, BF16 = jnp.float32, jnp.bfloat16
 
 
-def kernel(a, g, out, av, gv, acc, s0s, s0r, sbuf, ra, rb, rc, fbuf,
-           a_sem, g_sem, s0_ssem, s0_rsem, r_ssem, ra_sem, rb_sem, rc_sem, b_ssem, b_rsem, p_rsem):
+PARTS = 8
+
+
+def kernel(a, g, out, av, gv, acc, s0r, sbuf, ra, rb, rc, fbuf,
+           a_sem, g_sem, first_sem, s0_ssem, s0_rsem, r_ssem, ra_sem, rb_sem, rc_sem, b_ssem, b_rsem, p_rsem):
     matrices, tokens, depth = a.shape
     per = g.shape[2] // CW
     blocks = matrices * per
@@ -61,7 +64,7 @@
         return pltpu.make_async_copy(g.at[i // per, :, columns], gv.at[i % 2], g_sem.at[i % 2])
 
     def s0(i):
-        return remote(s0s.at[i % WF], s0r.at[i % WF], s0_ssem.at[i % WF], s0_rsem.at[i % WF], partner)
+        return remote(acc.at[i % WS, rows((1 - core) * half, half)], s0r.at[i % WF], s0_ssem.at[i % WF], s0_rsem.at[i % WF], partner)
 
     def to_a(j, start, size, to, k):
         return remote(sbuf.at[j % WS, rows(start, size)], ra.at[j % WL, pl.ds(0, size)],
@@ -75,20 +78,16 @@
         return remote(sbuf.at[j % WS, rows(start, q)], rc.at[j % WS],
                       r_ssem.at[2, j % WF], rc_sem.at[j % WS], to)
 
-    def finished(j, r, zz, slot, kind, to, src=None):
-        at = place(j, piece(r, zz))
+    def finished(j, start, size, slot, kind, to, src=None):
+        at = place(j, start, size)
         return remote(at if src is None else src, at, b_ssem.at[slot, j % WF], b_rsem.at[kind, j % WL], to)
 
-    def beside(j, r, zz, slot, src=None):
-        at = place(j, piece(r, zz))
-        return remote(at if src is None else src, at, b_ssem.at[slot, j % WF], p_rsem.at[r * 2 + zz, j % WL], partner)
-
-    def arrived(j, r, zz, kind):
-        finished(j, r, zz, 0, kind, partner).wait_recv()
-
-    def sent(j, *slots):
-        for slot in slots:
-            finished(j, 0, 0, slot, 0, partner).wait_send()
+    def beside(j, which):
+        at = place(j, which * half, half)
+        return remote(at, at, b_ssem.at[7, j % WF], p_rsem.at[j % WL], partner)
+
+    def kept(j):
+        return pltpu.make_async_copy(fbuf.at[j % WF], place(j, piece(y, zi)), b_ssem.at[4, j % WF])
 
     def mine(j, start, size):
         return acc.at[j % WS, rows(core * half + start, size)]
@@ -96,20 +95,41 @@
     def plus(x, y):
         return x[...] + y[...].astype(F32)
 
+    def first_loads(k):
+        depths = pl.ds(k * (tokens // PARTS), tokens // PARTS)
+        return (pltpu.make_async_copy(a.at[0, depths], av.at[0, depths], first_sem.at[0, k]),
+                pltpu.make_async_copy(g.at[0, depths, pl.ds(0, CW)], gv.at[0, depths], first_sem.at[1, k]))
+
+    def product(x, w):
+        return lax.dot_general(x, w, (((0,), (0,)), ((), ())), preferred_element_type=F32)
+
     def multiply(i):
-        g_load(i).wait()
-
-        @pl.when(i % per == 0)
-        def _():
-            a_load(i // per).wait()
-
-        @pl.when(both(i % per == 0, i // per + 1 < matrices))
-        def _():
-            a_load(i // per + 1).start()
-
-        acc[i % WS] = lax.dot_general(av[(i // per) % 2], gv[i % 2], (((0,), (0,)), ((), ())),
-                                      preferred_element_type=F32)
-        s0s[i % WF] = acc[i % WS, rows((1 - core) * half, half)].astype(BF16)
+        @pl.when(i == 0)
+        def _():
+            acc[0] = jnp.zeros(acc.shape[1:], F32)
+
+            def part(k, carry):
+                for load in first_loads(k):
+                    load.wait()
+                depths = pl.ds(k * (tokens // PARTS), tokens // PARTS)
+                acc[0] += product(av[0, depths], gv[0, depths])
+                return carry
+
+            lax.fori_loop(0, PARTS, part, 0)
+
+        @pl.when(i > 0)
+        def _():
+            g_load(i).wait()
+
+            @pl.when(i % per == 0)
+            def _():
+                a_load(i // per).wait()
+
+            @pl.when(both(i % per == 1, i // per + 1 < matrices))
+            def _():
+                a_load(i // per + 1).start()
+
+            acc[i % WS] = product(av[(i // per) % 2], gv[i % 2])
 
         @pl.when(i + 2 < blocks)
         def _():
@@ -196,112 +216,87 @@
             to_c(j, 0, partner).wait()
             f = fbuf.at[j % WF]
             f[...] = plus(acc.at[j % WS, rows(piece(y, zi), q)], rc.at[j % WS]).astype(BF16)
-            finished(j, y, zi, 0, 0, other, f).start()
-            finished(j, y, zi, 1, 1, across, f).start()
-            finished(j, y, zi, 2, 0, side, f).start()
-            beside(j, y, zi, 3, f).start()
-            pltpu.make_async_copy(f, place(j, piece(y, zi)), b_ssem.at[4, j % WF]).start()
+
+            @pl.when(yf)
+            def _():
+                finished(j, piece(y, zi), q, 0, 0, other, f).start()
+
+            @pl.when(zf)
+            def _():
+                finished(j, piece(y, zi), q, 0, 0, across, f).start()
+                finished(j, piece(y, zi), q, 1, 1, other, f).start()
+                finished(j, piece(y, zi), q, 2, 0, side, f).start()
+
+            kept(j).start()
 
     def stage5(j):
         @pl.when(mid)
         def _():
-            sent(j, 0, 1, 2, 3)
-            pltpu.make_async_copy(fbuf.at[j % WF], place(j, piece(y, zi)), b_ssem.at[4, j % WF]).wait()
-            arrived(j, y, 1 - zi, 0)
-
-            @pl.when(yf)
-            def _():
-                finished(j, y, 1 - zi, 5, 1, side).start()
-                finished(j, y, 1 - zi, 6, 2, across).start()
-
-            @pl.when(zf)
-            def _():
-                finished(j, y, 1 - zi, 5, 2, side).start()
-
-            beside(j, y, 1 - zi, 7).start()
-            arrived(j, 1 - y, zi, 1)
-
-            @pl.when(zf)
-            def _():
-                finished(j, 1 - y, zi, 6, 2, other).start()
-                finished(j, 1 - y, zi, 9, 1, side).start()
-
-            beside(j, 1 - y, zi, 8).start()
+            kept(j).wait()
+            finished(j, 0, q, 0, 0, partner).wait()
+
+        @pl.when(both(yf, mid))
+        def _():
+            finished(j, y * quarter, quarter, 5, 0, side).start()
+            finished(j, y * quarter, quarter, 6, 1, across).start()
+
+        @pl.when(both(zf, mid))
+        def _():
+            finished(j, piece(1 - y, zi), q, 5, 2, other).start()
+            finished(j, 0, q, 1, 1, partner).wait()
+            finished(j, piece(y, 1 - zi), q, 6, 1, side).start()
+            finished(j, 0, q, 2, 0, partner).wait_send()
+
+        @pl.when(both(zf, end))
+        def _():
+            finished(j, 0, q, 0, 0, partner).wait_recv()
+            finished(j, piece(y, zi), q, 5, 2, across).start()
+
+    def stage6(j):
+        @pl.when(both(yf, mid))
+        def _():
+            finished(j, 0, quarter, 5, 1, partner).wait()
+            finished(j, 0, quarter, 6, 1, partner).wait_send()
+
+        @pl.when(both(zf, mid))
+        def _():
+            finished(j, 0, q, 5, 2, partner).wait()
+            finished(j, 0, q, 6, 2, partner).wait_send()
+
+        @pl.when(mid)
+        def _():
+            beside(j, core).start()
+
+        @pl.when(both(yf, end))
+        def _():
+            finished(j, 0, quarter, 6, 0, partner).wait_recv()
+            finished(j, y * quarter, quarter, 6, 1, across).start()
+
+        @pl.when(both(zf, end))
+        def _():
+            finished(j, 0, q, 5, 1, partner).wait()
+            finished(j, piece(y, 1 - zi), q, 6, 3, across).start()
+
+    def stage7(j):
+        @pl.when(both(yf, end))
+        def _():
+            finished(j, 0, quarter, 6, 1, partner).wait()
+
+        @pl.when(both(zf, end))
+        def _():
+            finished(j, 0, q, 6, 2, partner).wait()
+            finished(j, 0, q, 6, 3, partner).wait_recv()
 
         @pl.when(end)
         def _():
-            arrived(j, y, zi, 0)
-
-            @pl.when(yf)
-            def _():
-                finished(j, y, zi, 6, 2, across).start()
-
-            beside(j, y, zi, 5).start()
-
-    def stage6(j):
-        @pl.when(mid)
-        def _():
-            sent(j, 5, 6, 7, 8)
-
-            @pl.when(zf)
-            def _():
-                sent(j, 9)
-
-            arrived(j, 1 - y, 1 - zi, 2)
-
-            @pl.when(zf)
-            def _():
-                finished(j, 1 - y, 1 - zi, 11, 3, side).start()
-
-            beside(j, 1 - y, 1 - zi, 10).start()
-
-        @pl.when(end)
-        def _():
-            sent(j, 5)
-
-        @pl.when(both(end, yf))
-        def _():
-            sent(j, 6)
-            arrived(j, y, 1 - zi, 1)
-            finished(j, y, 1 - zi, 11, 3, across).start()
-            beside(j, y, 1 - zi, 10).start()
-            arrived(j, 1 - y, zi, 2)
-            beside(j, 1 - y, zi, 12).start()
-
-        @pl.when(both(end, zf))
-        def _():
-            arrived(j, 1 - y, zi, 1)
-            beside(j, 1 - y, zi, 10).start()
-            arrived(j, y, 1 - zi, 2)
-            beside(j, y, 1 - zi, 12).start()
-
-    def stage7(j):
-        sent(j, 10)
-
-        @pl.when(both(zf, mid))
-        def _():
-            sent(j, 11)
-
-        @pl.when(both(yf, end))
-        def _():
-            sent(j, 11)
-
-        @pl.when(end)
-        def _():
-            sent(j, 12)
-            arrived(j, 1 - y, 1 - zi, 3)
-            beside(j, 1 - y, 1 - zi, 13).start()
+            beside(j, core).start()
 
     def stage8(j):
-        @pl.when(end)
-        def _():
-            sent(j, 13)
-
-        for k in range(4):
-            beside(j, k // 2, k % 2, 0).wait_recv()
-
-    a_load(0).start()
-    g_load(0).start()
+        beside(j, 1 - core).wait()
+
+    for k in range(PARTS):
+        for load in first_loads(k):
+            load.start()
     g_load(1).start()
 
     barrier = pltpu.get_barrier_semaphore()
@@ -333,6 +328,25 @@
         return carry
 
     lax.fori_loop(0, blocks + LAG[-1], tick, 0)
+
+
+def place_kernel(x, o, held, in_sem, out_sem):
+    matrices, bands, size, _ = held.shape
+    every = [(n, b) for n in range(matrices) for b in range(bands)]
+
+    def load(n, b):
+        return pltpu.make_async_copy(x.at[n, pl.ds(b * size, size)], held.at[n, b], in_sem.at[n, b])
+
+    def store(n, b):
+        return pltpu.make_async_copy(held.at[n, b], o.at[n, pl.ds(b * size, size)], out_sem.at[n, b])
+
+    for nb in every:
+        load(*nb).start()
+    for nb in every:
+        load(*nb).wait()
+        store(*nb).start()
+    for nb in every:
+        store(*nb).wait()
 
 
 def solution(mesh):
@@ -341,7 +355,7 @@
         width = g.shape[3]
         q = depth // 8
         dma = pltpu.SemaphoreType.DMA
-        return pl.pallas_call(
+        sums = pl.pallas_call(
             kernel,
             out_shape=jax.ShapeDtypeStruct((matrices, depth, width), BF16),
             in_specs=[pl.BlockSpec(memory_space=pl.ANY)] * 2,
@@ -350,15 +364,14 @@
                 pltpu.VMEM((2, tokens, depth), BF16),
                 pltpu.VMEM((2, tokens, CW), BF16),
                 pltpu.VMEM((WS, depth, CW), F32),
-                pltpu.VMEM((WF, 4 * q, CW), BF16),
-                pltpu.VMEM((WF, 4 * q, CW), BF16),
+                pltpu.VMEM((WF, 4 * q, CW), F32),
                 pltpu.VMEM((WS, 4 * q, CW), BF16),
                 pltpu.VMEM((WL, 4 * q, CW), BF16),
                 pltpu.VMEM((WS, 2 * q, CW), BF16),
                 pltpu.VMEM((WS, q, CW), BF16),
                 pltpu.VMEM((WF, q, CW), BF16),
-                dma((2,)), dma((2,)), dma((WF,)), dma((WF,)), dma((3, WF)), dma((WL,)), dma((WS,)), dma((WS,)),
-                dma((14, WF)), dma((4, WL)), dma((4, WL)),
+                dma((2,)), dma((2,)), dma((2, PARTS)), dma((WF,)), dma((WF,)), dma((3, WF)), dma((WL,)), dma((WS,)), dma((WS,)),
+                dma((8, WF)), dma((4, WL)), dma((WL,)),
             ],
             compiler_params=pltpu.CompilerParams(
                 collective_id=0, has_side_effects=True, vmem_limit_bytes=VMEM_LIMIT),
@@ -367,6 +380,17 @@
                 bytes_accessed=2 * matrices * (tokens * (depth + width) + depth * width), transcendentals=0),
             name="sums",
         )(a[0], g[0])
+        bands = (matrices, 4, depth // 4, width)
+        return pl.pallas_call(
+            place_kernel,
+            out_shape=jax.ShapeDtypeStruct(sums.shape, BF16),
+            in_specs=[pl.BlockSpec(memory_space=pl.ANY)],
+            out_specs=pl.BlockSpec(memory_space=pl.ANY),
+            scratch_shapes=[pltpu.VMEM(bands, BF16), dma(bands[:2]), dma(bands[:2])],
+            compiler_params=pltpu.CompilerParams(vmem_limit_bytes=VMEM_LIMIT),
+            cost_estimate=pl.CostEstimate(flops=0, bytes_accessed=4 * matrices * depth * width, transcendentals=0),
+            name="place",
+        )(sums)
 
     return jax.shard_map(
         step, mesh=mesh,

time: 297 us -> 279 us (0.939)
  local copies, waits for them, and re-layouts: 19.8 us -> 0 us
    unnamed x1 -> x0, local copies, waits for them, and re-layouts: 19.8 us -> none
    pallas_call x0 -> x1, Pallas kernels: none -> 16.1 us  [step(): pl.pallas_call(place_kernel, out_shape=jax.ShapeDtypeStruct(sums.shape, B...]
    pallas_call x1, Pallas kernels: 277 us -> 263 us  [step(): pl.pallas_call(kernel, out_shape=jax.ShapeDtypeStruct((matrices, depth, w...]
where the time goes in v2:
time: 279 us
  Pallas kernels  279 us (100%)
    pallas_call x1, Pallas kernels, step(): pl.pallas_call(kernel, out_shape=jax.ShapeDtypeStruct((matrices, depth, w...  263 us
    pallas_call x1, Pallas kernels, step(): pl.pallas_call(place_kernel, out_shape=jax.ShapeDtypeStruct(sums.shape, B...  16.1 us

profile of v2, /device:TPU:0, one launch (start us, length us, event | category | flops | bytes accessed | tf_op | source)
XLA Modules:
  0.0 278.9 jit_solution(1478887493973686155)
XLA Ops:
  0.0 262.9 %sums.1.x = bf16[4,1024,2816]{2,1,0:T(8,128)(2,1)} custom-call(bf16[4,8192,1024]{2,1,0:T(8,128)(2,1)} %bitcast.a, bf16[4,8192,2816]{2,1,0:T(8,128)(2,1)} %bitcast.1.g), custom_call_target="tpu_custom_call" | custom-call | flops 188978561024 | bytes 274726912 | tf_op jit(solution)/shard_map/sums/pallas_call | solution.py:358
  262.9 16.1 %place.1 = bf16[4,1024,2816]{2,1,0:T(8,128)(2,1)} custom-call(bf16[4,1024,2816]{2,1,0:T(8,128)(2,1)} %sums.1.x), custom_call_target="tpu_custom_call" | custom-call | bytes 46137344 | tf_op jit(solution)/shard_map/place/pallas_call | solution.py:384

commit v3 on v2

--- a/solution.py
+++ b/solution.py
@@ -9,8 +9,9 @@
 
 CW = 256
 LAG = (1, 2, 3, 4, 5, 7, 9, 10)
-WL = 16
+WL = 12
 WS = 8
+WA = 6
 WF = 4
 VMEM_LIMIT = 67043328
 F32, BF16 = jnp.float32, jnp.bfloat16
@@ -19,7 +20,7 @@
 PARTS = 8
 
 
-def kernel(a, g, out, av, gv, acc, s0r, sbuf, ra, rb, rc, fbuf,
+def kernel(a, g, out, av, gv, acc, s0r, sbuf, ra, rb, rc, fin,
            a_sem, g_sem, first_sem, s0_ssem, s0_rsem, r_ssem, ra_sem, rb_sem, rc_sem, b_ssem, b_rsem, p_rsem):
     matrices, tokens, depth = a.shape
     per = g.shape[2] // CW
@@ -45,7 +46,7 @@
         return pl.ds(pl.multiple_of(start, q), size)
 
     def piece(r, zz):
-        return core * half + r * (quarter - q * core) + zz * (q + q * core)
+        return r * (quarter - q * core) + zz * (q + q * core)
 
     def place(j, start, size=q):
         columns = pl.ds(pl.multiple_of((j % per) * CW, CW), CW)
@@ -64,36 +65,38 @@
         return pltpu.make_async_copy(g.at[i // per, :, columns], gv.at[i % 2], g_sem.at[i % 2])
 
     def s0(i):
-        return remote(acc.at[i % WS, rows((1 - core) * half, half)], s0r.at[i % WF], s0_ssem.at[i % WF], s0_rsem.at[i % WF], partner)
+        return remote(acc.at[i % WA, rows((1 - core) * half, half)], s0r.at[i % WA], s0_ssem.at[i % WA], s0_rsem.at[i % WA], partner)
 
     def to_a(j, start, size, to, k):
-        return remote(sbuf.at[j % WS, rows(start, size)], ra.at[j % WL, pl.ds(0, size)],
+        return remote(sbuf.at[j % WA, rows(start, size)], ra.at[j % WL, pl.ds(0, size)],
                       r_ssem.at[k, j % WF], ra_sem.at[j % WL], to)
 
     def to_b(j, start, to, k):
-        return remote(sbuf.at[j % WS, rows(start, quarter)], rb.at[j % WS],
+        return remote(sbuf.at[j % WA, rows(start, quarter)], rb.at[j % WS],
                       r_ssem.at[k, j % WF], rb_sem.at[j % WS], to)
 
     def to_c(j, start, to):
-        return remote(sbuf.at[j % WS, rows(start, q)], rc.at[j % WS],
+        return remote(sbuf.at[j % WA, rows(start, q)], rc.at[j % WS],
                       r_ssem.at[2, j % WF], rc_sem.at[j % WS], to)
 
-    def finished(j, start, size, slot, kind, to, src=None):
-        at = place(j, start, size)
-        return remote(at if src is None else src, at, b_ssem.at[slot, j % WF], b_rsem.at[kind, j % WL], to)
+    def finished(j, start, size, slot, kind, to):
+        at = fin.at[j % WL, rows(start, size)]
+        return remote(at, at, b_ssem.at[slot, j % WF], b_rsem.at[kind, j % WL], to)
 
     def beside(j, which):
-        at = place(j, which * half, half)
-        return remote(at, at, b_ssem.at[7, j % WF], p_rsem.at[j % WL], partner)
+        return remote(fin.at[j % WL], place(j, which * half, half), b_ssem.at[7, j % WF], p_rsem.at[j % WL], partner)
 
     def kept(j):
-        return pltpu.make_async_copy(fbuf.at[j % WF], place(j, piece(y, zi)), b_ssem.at[4, j % WF])
+        return pltpu.make_async_copy(fin.at[j % WL], place(j, core * half, half), b_ssem.at[4, j % WF])
 
     def mine(j, start, size):
-        return acc.at[j % WS, rows(core * half + start, size)]
-
-    def plus(x, y):
-        return x[...] + y[...].astype(F32)
+        return acc.at[j % WA, rows(core * half + start, size)]
+
+    def plus(x, *others):
+        return functools.reduce(lambda total, y: total + y[...].astype(F32), others, x[...])
+
+    def beside_sum(j, start, size):
+        return s0r.at[j % WA, rows(start, size)]
 
     def first_loads(k):
         depths = pl.ds(k * (tokens // PARTS), tokens // PARTS)
@@ -103,33 +106,31 @@
     def product(x, w):
         return lax.dot_general(x, w, (((0,), (0,)), ((), ())), preferred_element_type=F32)
 
+    def multiply_first():
+        acc[0] = jnp.zeros(acc.shape[1:], F32)
+
+        def part(k, carry):
+            for load in first_loads(k):
+                load.wait()
+            depths = pl.ds(k * (tokens // PARTS), tokens // PARTS)
+            acc[0] += product(av[0, depths], gv[0, depths])
+            return carry
+
+        lax.fori_loop(0, PARTS, part, 0)
+        g_load(2).start()
+
     def multiply(i):
-        @pl.when(i == 0)
-        def _():
-            acc[0] = jnp.zeros(acc.shape[1:], F32)
-
-            def part(k, carry):
-                for load in first_loads(k):
-                    load.wait()
-                depths = pl.ds(k * (tokens // PARTS), tokens // PARTS)
-                acc[0] += product(av[0, depths], gv[0, depths])
-                return carry
-
-            lax.fori_loop(0, PARTS, part, 0)
-
-        @pl.when(i > 0)
-        def _():
-            g_load(i).wait()
-
-            @pl.when(i % per == 0)
-            def _():
-                a_load(i // per).wait()
-
-            @pl.when(both(i % per == 1, i // per + 1 < matrices))
-            def _():
-                a_load(i // per + 1).start()
-
-            acc[i % WS] = product(av[(i // per) % 2], gv[i % 2])
+        g_load(i).wait()
+
+        @pl.when(i % per == 0)
+        def _():
+            a_load(i // per).wait()
+
+        @pl.when(both(i % per == 1, i // per + 1 < matrices))
+        def _():
+            a_load(i // per + 1).start()
+
+        acc[i % WA] = product(av[(i // per) % 2], gv[i % 2])
 
         @pl.when(i + 2 < blocks)
         def _():
@@ -139,23 +140,18 @@
 
     def stage1(j):
         s0(j).wait()
-        theirs = s0r.at[j % WF]
+        theirs = s0r.at[j % WA]
 
         @pl.when(yf)
         def _():
-            away, own = (1 - y) * quarter, y * quarter
-            sbuf[j % WS, rows(away, quarter)] = plus(mine(j, away, quarter), theirs.at[rows(away, quarter)]).astype(BF16)
+            away = (1 - y) * quarter
+            sbuf[j % WA, rows(away, quarter)] = plus(mine(j, away, quarter), theirs.at[rows(away, quarter)]).astype(BF16)
             to_b(j, away, across, 0).start()
-            mine(j, own, quarter)[...] = plus(mine(j, own, quarter), theirs.at[rows(own, quarter)])
 
         @pl.when(both(zf, end))
         def _():
-            sbuf[j % WS] = plus(mine(j, 0, half), theirs).astype(BF16)
+            sbuf[j % WA] = plus(mine(j, 0, half), theirs).astype(BF16)
             to_a(j, 0, half, side, 0).start()
-
-        @pl.when(both(zf, mid))
-        def _():
-            mine(j, 0, half)[...] = plus(mine(j, 0, half), theirs)
 
     def stage2(j):
         @pl.when(yf)
@@ -165,12 +161,12 @@
 
             @pl.when(end)
             def _():
-                sbuf[j % WS, rows(own, quarter)] = plus(mine(j, own, quarter), rb.at[j % WS]).astype(BF16)
+                sbuf[j % WA, rows(own, quarter)] = plus(mine(j, own, quarter), beside_sum(j, own, quarter), rb.at[j % WS]).astype(BF16)
                 to_a(j, own, quarter, side, 1).start()
 
             @pl.when(mid)
             def _():
-                mine(j, own, quarter)[...] = plus(mine(j, own, quarter), rb.at[j % WS])
+                mine(j, own, quarter)[...] = plus(mine(j, own, quarter), beside_sum(j, own, quarter), rb.at[j % WS])
 
         @pl.when(both(zf, end))
         def _():
@@ -181,9 +177,11 @@
             to_a(j, 0, half, side, 0).wait_recv()
             away, own = (1 - zi) * quarter, zi * quarter
             theirs = ra.at[j % WL]
-            sbuf[j % WS, rows(away, quarter)] = plus(mine(j, away, quarter), theirs.at[rows(away, quarter)]).astype(BF16)
+            sbuf[j % WA, rows(away, quarter)] = plus(
+                mine(j, away, quarter), beside_sum(j, away, quarter), theirs.at[rows(away, quarter)]).astype(BF16)
             to_b(j, away, other, 1).start()
-            mine(j, own, quarter)[...] = plus(mine(j, own, quarter), theirs.at[rows(own, quarter)])
+            mine(j, own, quarter)[...] = plus(
+                mine(j, own, quarter), beside_sum(j, own, quarter), theirs.at[rows(own, quarter)])
 
     def stage3(j):
         @pl.when(both(yf, end))
@@ -195,7 +193,7 @@
             to_a(j, y * quarter, quarter, side, 1).wait_recv()
             away, own = (1 - zi) * q, zi * q
             theirs = ra.at[j % WL]
-            sbuf[j % WS, rows(y * quarter + away, q)] = plus(
+            sbuf[j % WA, rows(y * quarter + away, q)] = plus(
                 mine(j, y * quarter + away, q), theirs.at[rows(away, q)]).astype(BF16)
             to_c(j, y * quarter + away, other).start()
             mine(j, y * quarter + own, q)[...] = plus(mine(j, y * quarter + own, q), theirs.at[rows(own, q)])
@@ -205,7 +203,7 @@
             to_b(j, (1 - zi) * quarter, other, 1).wait()
             away, own = (1 - y) * q, y * q
             theirs = rb.at[j % WS]
-            sbuf[j % WS, rows(zi * quarter + away, q)] = plus(
+            sbuf[j % WA, rows(zi * quarter + away, q)] = plus(
                 mine(j, zi * quarter + away, q), theirs.at[rows(away, q)]).astype(BF16)
             to_c(j, zi * quarter + away, across).start()
             mine(j, zi * quarter + own, q)[...] = plus(mine(j, zi * quarter + own, q), theirs.at[rows(own, q)])
@@ -214,25 +212,21 @@
         @pl.when(mid)
         def _():
             to_c(j, 0, partner).wait()
-            f = fbuf.at[j % WF]
-            f[...] = plus(acc.at[j % WS, rows(piece(y, zi), q)], rc.at[j % WS]).astype(BF16)
+            fin[j % WL, rows(piece(y, zi), q)] = plus(mine(j, piece(y, zi), q), rc.at[j % WS]).astype(BF16)
 
             @pl.when(yf)
             def _():
-                finished(j, piece(y, zi), q, 0, 0, other, f).start()
+                finished(j, piece(y, zi), q, 0, 0, other).start()
 
             @pl.when(zf)
             def _():
-                finished(j, piece(y, zi), q, 0, 0, across, f).start()
-                finished(j, piece(y, zi), q, 1, 1, other, f).start()
-                finished(j, piece(y, zi), q, 2, 0, side, f).start()
-
-            kept(j).start()
+                finished(j, piece(y, zi), q, 0, 0, across).start()
+                finished(j, piece(y, zi), q, 1, 1, other).start()
+                finished(j, piece(y, zi), q, 2, 0, side).start()
 
     def stage5(j):
         @pl.when(mid)
         def _():
-            kept(j).wait()
             finished(j, 0, q, 0, 0, partner).wait()
 
         @pl.when(both(yf, mid))
@@ -266,6 +260,7 @@
         @pl.when(mid)
         def _():
             beside(j, core).start()
+            kept(j).start()
 
         @pl.when(both(yf, end))
         def _():
@@ -290,9 +285,11 @@
         @pl.when(end)
         def _():
             beside(j, core).start()
+            kept(j).start()
 
     def stage8(j):
         beside(j, 1 - core).wait()
+        kept(j).wait()
 
     for k in range(PARTS):
         for load in first_loads(k):
@@ -310,12 +307,19 @@
     @pl.when(mid)
     def _():
         hello(other)
+
+    multiply_first()
+
+    @pl.when(mid)
+    def _():
         pl.semaphore_wait(barrier, 4)
 
     @pl.when(end)
     def _():
         pl.semaphore_wait(barrier, 3)
 
+    s0(0).start()
+
     stages = (stage1, stage2, stage3, stage4, stage5, stage6, stage7, stage8)
 
     def tick(i, carry):
@@ -327,7 +331,7 @@
             pl.when(both(i >= lag, i < blocks + lag))(functools.partial(stage, i - lag))
         return carry
 
-    lax.fori_loop(0, blocks + LAG[-1], tick, 0)
+    lax.fori_loop(1, blocks + LAG[-1], tick, 0)
 
 
 def place_kernel(x, o, held, in_sem, out_sem):
@@ -363,14 +367,14 @@
             scratch_shapes=[
                 pltpu.VMEM((2, tokens, depth), BF16),
                 pltpu.VMEM((2, tokens, CW), BF16),
-                pltpu.VMEM((WS, depth, CW), F32),
-                pltpu.VMEM((WF, 4 * q, CW), F32),
-                pltpu.VMEM((WS, 4 * q, CW), BF16),
+                pltpu.VMEM((WA, depth, CW), F32),
+                pltpu.VMEM((WA, 4 * q, CW), F32),
+                pltpu.VMEM((WA, 4 * q, CW), BF16),
                 pltpu.VMEM((WL, 4 * q, CW), BF16),
                 pltpu.VMEM((WS, 2 * q, CW), BF16),
                 pltpu.VMEM((WS, q, CW), BF16),
-                pltpu.VMEM((WF, q, CW), BF16),
-                dma((2,)), dma((2,)), dma((2, PARTS)), dma((WF,)), dma((WF,)), dma((3, WF)), dma((WL,)), dma((WS,)), dma((WS,)),
+                pltpu.VMEM((WL, 4 * q, CW), BF16),
+                dma((2,)), dma((2,)), dma((2, PARTS)), dma((WA,)), dma((WA,)), dma((3, WF)), dma((WL,)), dma((WS,)), dma((WS,)),
                 dma((8, WF)), dma((4, WL)), dma((WL,)),
             ],
             compiler_params=pltpu.CompilerParams(

time: 279 us -> 276 us (0.989)
  Pallas kernels: 279 us -> 275 us
    pallas_call x1, Pallas kernels: 263 us -> 259 us  [step(): pl.pallas_call(kernel, out_shape=jax.ShapeDtypeStruct((matrices, depth, w...]
where the time goes in v3:
time: 276 us; the launch traced here: 275 us
  Pallas kernels  275 us (100%)
    pallas_call x1, Pallas kernels, step(): pl.pallas_call(kernel, out_shape=jax.ShapeDtypeStruct((matrices, depth, w...  259 us
    pallas_call x1, Pallas kernels, step(): pl.pallas_call(place_kernel, out_shape=jax.ShapeDtypeStruct(sums.shape, B...  16.1 us

profile of v3, /device:TPU:0, one launch (start us, length us, event | category | flops | bytes accessed | tf_op | source)
XLA Modules:
  0.0 275.4 jit_solution(15036394037354522696)
XLA Ops:
  0.0 259.3 %sums.1.x = bf16[4,1024,2816]{2,1,0:T(8,128)(2,1)} custom-call(bf16[4,8192,1024]{2,1,0:T(8,128)(2,1)} %bitcast.a, bf16[4,8192,2816]{2,1,0:T(8,128)(2,1)} %bitcast.1.g), custom_call_target="tpu_custom_call" | custom-call | flops 188978561024 | bytes 274726912 | tf_op jit(solution)/shard_map/sums/pallas_call | solution.py:362
  259.3 16.1 %place.1 = bf16[4,1024,2816]{2,1,0:T(8,128)(2,1)} custom-call(bf16[4,1024,2816]{2,1,0:T(8,128)(2,1)} %sums.1.x), custom_call_target="tpu_custom_call" | custom-call | bytes 46137344 | tf_op jit(solution)/shard_map/place/pallas_call | solution.py:388
